TPU v7x, 32 devices: a whole 2x2x4 slice. The times are simulated.
32 devices in a mesh: dp: 4 (over y, x), fsdp: 8 (over z, core).
Axes of the slice: x: 2, y: 2, z: 4, core: 2. Of those that a mesh axis runs over, the one named last changes fastest.
Arguments:
- hidden_in: bfloat16 [32, 8192], P(('dp', 'fsdp')), may hold values from -6 to 6
- lengths: int32 [32], P(('dp', 'fsdp')), may hold values from 1 to 511
- key_cache: bfloat16 [32, 512, 1024], P(('dp', 'fsdp')), may hold values from -68 to 68
- value_cache: bfloat16 [32, 512, 1024], P(('dp', 'fsdp')), may hold values from -6 to 6
- attn_gain: bfloat16 [8192], replicated, may hold values from 0.5 to 1.5
- w_qkv: bfloat16 [8192, 10240], P('fsdp', 'dp'), may hold values from -0.0625 to 0.0625
- w_out: bfloat16 [8192, 8192], P('fsdp', 'dp'), may hold values from -0.5 to 0.5
- mlp_gain: bfloat16 [8192], replicated, may hold values from 0.5 to 1.5
- w_gate: bfloat16 [8192, 28672], P('dp', 'fsdp'), may hold values from -0.0625 to 0.0625
- w_up: bfloat16 [8192, 28672], P('dp', 'fsdp'), may hold values from -0.0625 to 0.0625
- w_down: bfloat16 [28672, 8192], P('fsdp', 'dp'), may hold values from -0.03125 to 0.03125
Outputs:
- hidden_out: bfloat16 [32, 8192], P(('dp', 'fsdp'))
- new_keys: bfloat16 [32, 1024], P(('dp', 'fsdp'))
- new_values: bfloat16 [32, 1024], P(('dp', 'fsdp'))
Inputs may be any that keep to these rules, and one draw needn't show every extreme that they name: Each sequence's number of cached positions; its new token takes position lengths.
All inputs are finite; a program needn't handle non-finite values.
Results may differ from a plain program's by a relative error of at most 0.012.
The roundings to bfloat16 on the way count: a program that leaves them out, or rounds other values in their place, can miss the bound.
Values may be sent and summed in bfloat16 or wider, within the bound.
A program may use at most 128 MiB of HBM per device.

v0:
```python
import jax
import jax.numpy as jnp
from jax import lax
from jax.sharding import PartitionSpec as P

HEADS = 64
KV_HEADS = 8
HD = 128
rope_base = 500000.0
norm_eps = 1e-05


def rms_scale(values, gain_row):
    mean_square = jnp.mean(values * values, axis=-1, keepdims=True)
    return values * lax.rsqrt(mean_square + norm_eps) * gain_row.astype(jnp.float32)


def rotate(values, positions):
    half_dim = values.shape[-1] // 2
    frequency = rope_base ** (-2.0 * jnp.arange(half_dim, dtype=jnp.float32) / values.shape[-1])
    angles = positions.astype(jnp.float32)[:, None] * frequency[None, :]
    cosine = jnp.cos(angles)[:, None, :]
    sine_wave = jnp.sin(angles)[:, None, :]
    lower_half = values[..., :half_dim]
    upper_half = values[..., half_dim:]
    return jnp.concatenate(
        [
            lower_half * cosine - upper_half * sine_wave,
            upper_half * cosine + lower_half * sine_wave,
        ],
        axis=-1,
    )


def attend(queries, new_keys, new_values, key_cache, value_cache, lengths):
    seq_count, context, kv_width = key_cache.shape
    kv_heads = new_keys.shape[1]
    head_dim = new_keys.shape[2]
    score_scale = head_dim ** (-0.5)
    key_rows = key_cache.reshape(seq_count, context, kv_heads, head_dim)
    value_rows = value_cache.reshape(seq_count, context, kv_heads, head_dim)
    grouped = queries.reshape(seq_count, kv_heads, -1, head_dim)
    scores = (
        jnp.einsum("skgd,sckd->skgc", grouped, key_rows, preferred_element_type=jnp.float32)
        * score_scale
    )
    is_valid = (
        jnp.arange(context, dtype=jnp.int32)[None, None, None, :] < lengths[:, None, None, None]
    )
    scores = jnp.where(is_valid, scores, -1e30)
    own_score = (
        jnp.einsum("skgd,skd->skg", grouped, new_keys, preferred_element_type=jnp.float32)
        * score_scale
    )
    row_max = jnp.maximum(jnp.max(scores, axis=-1), own_score)
    weights = jnp.exp(scores - row_max[..., None])
    own_weight = jnp.exp(own_score - row_max)
    denom_sum = jnp.sum(weights, axis=-1) + own_weight
    probability = (weights / denom_sum[..., None]).astype(jnp.bfloat16)
    own_prob = (own_weight / denom_sum).astype(jnp.bfloat16)
    mixed = jnp.einsum(
        "skgc,sckd->skgd", probability, value_rows, preferred_element_type=jnp.float32
    )
    mixed = (
        mixed
        + own_prob.astype(jnp.float32)[..., None] * new_values.astype(jnp.float32)[:, :, None, :]
    )
    return mixed.astype(jnp.bfloat16).reshape(seq_count, -1)


def quarter_split(values, dp_size, fsdp_size):
    seq_count = values.shape[0]
    return values.reshape(seq_count, fsdp_size, dp_size, -1)


def quarter_join(moved, dp_size):
    return moved.reshape(dp_size, moved.shape[0] // dp_size, -1)[None]


def on_device(
    hidden_in,
    lengths,
    key_cache,
    value_cache,
    attn_gain,
    w_qkv,
    w_out,
    mlp_gain,
    w_gate,
    w_up,
    w_down,
):
    seq_count = hidden_in.shape[0]
    q_width = HEADS * HD
    kv_width = KV_HEADS * HD
    dp_size = lax.axis_size("dp")
    fsdp_size = lax.axis_size("fsdp")
    residual = hidden_in.astype(jnp.float32)
    normed = rms_scale(residual, attn_gain).astype(jnp.bfloat16)
    qkv_tile = lax.all_to_all(
        lax.all_to_all(w_qkv, "dp", split_axis=0, concat_axis=1, tiled=True),
        "fsdp",
        split_axis=1,
        concat_axis=0,
        tiled=True,
    )
    qkv_moved = lax.all_to_all(
        quarter_split(normed, dp_size, fsdp_size), "dp", split_axis=2, concat_axis=0, tiled=True
    )
    qkv_in = quarter_join(qkv_moved, dp_size)
    qkv_parts = jnp.einsum(
        "fpsk,kn->fpsn",
        lax.all_gather(qkv_in, "fsdp", axis=0, tiled=True),
        qkv_tile,
        preferred_element_type=jnp.float32,
    )
    qkv_share = lax.psum_scatter(qkv_parts, "dp", scatter_dimension=1, tiled=True)
    projected = lax.all_to_all(qkv_share, "fsdp", split_axis=0, concat_axis=3, tiled=True)[0, 0]
    queries = rotate(projected[:, :q_width].reshape(seq_count, HEADS, HD), lengths).astype(
        jnp.bfloat16
    )
    new_keys = rotate(
        projected[:, q_width : q_width + kv_width].reshape(seq_count, KV_HEADS, HD), lengths
    ).astype(jnp.bfloat16)
    new_values = projected[:, q_width + kv_width :].astype(jnp.bfloat16)
    mixed = attend(
        queries,
        new_keys,
        new_values.reshape(seq_count, KV_HEADS, HD),
        key_cache,
        value_cache,
        lengths,
    )
    out_tile = lax.all_to_all(
        lax.all_to_all(w_out, "dp", split_axis=0, concat_axis=1, tiled=True),
        "fsdp",
        split_axis=1,
        concat_axis=0,
        tiled=True,
    )
    out_moved = lax.all_to_all(
        quarter_split(mixed, dp_size, fsdp_size), "dp", split_axis=2, concat_axis=0, tiled=True
    )
    out_in = quarter_join(out_moved, dp_size)
    out_parts = jnp.einsum(
        "fpsk,kn->fpsn",
        lax.all_gather(out_in, "fsdp", axis=0, tiled=True),
        out_tile,
        preferred_element_type=jnp.float32,
    )
    out_share = lax.psum_scatter(out_parts, "dp", scatter_dimension=1, tiled=True)
    attn_sum = lax.all_to_all(out_share, "fsdp", split_axis=0, concat_axis=3, tiled=True)[0, 0]
    residual_mid = residual + attn_sum
    normed_mid = rms_scale(residual_mid, mlp_gain).astype(jnp.bfloat16)
    mlp_in = lax.all_to_all(normed_mid[None], "dp", split_axis=2, concat_axis=0, tiled=True)
    pieces = lax.all_gather(mlp_in[None], "fsdp", axis=0, tiled=True)
    gate_part = jnp.einsum("fask,kn->fasn", pieces, w_gate, preferred_element_type=jnp.float32)
    up_part = jnp.einsum("fask,kn->fasn", pieces, w_up, preferred_element_type=jnp.float32)
    partials = jnp.stack([gate_part, up_part], axis=3)
    summed = lax.psum(partials.astype(jnp.bfloat16), "dp").astype(jnp.float32)
    activated = (jax.nn.silu(summed[:, :, :, 0]) * summed[:, :, :, 1]).astype(jnp.bfloat16)
    reduced_down = lax.psum_scatter(
        jnp.einsum("fask,kn->fasn", activated, w_down, preferred_element_type=jnp.float32),
        "fsdp",
        scatter_dimension=0,
        tiled=True,
    )
    down_sum = lax.all_to_all(
        reduced_down.astype(jnp.bfloat16), "dp", split_axis=1, concat_axis=3, tiled=True
    ).astype(reduced_down.dtype)[0, 0]
    hidden_out = (residual_mid + down_sum).astype(jnp.bfloat16)
    return (hidden_out, new_keys.reshape(seq_count, kv_width), new_values)


def solution(mesh):
    in_specs = (
        P(("dp", "fsdp"), None),
        P(("dp", "fsdp")),
        P(("dp", "fsdp"), None, None),
        P(("dp", "fsdp"), None, None),
        P(),
        P("fsdp", "dp"),
        P("fsdp", "dp"),
        P(),
        P("dp", "fsdp"),
        P("dp", "fsdp"),
        P("fsdp", "dp"),
    )
    out_specs = (P(("dp", "fsdp"), None), P(("dp", "fsdp"), None), P(("dp", "fsdp"), None))
    return jax.shard_map(
        on_device, mesh=mesh, in_specs=in_specs, out_specs=out_specs, check_vma=False
    )
```

profile of v0, /device:TPU:0, one launch (start us, length us, event | category | flops | bytes accessed | tf_op | source)
XLA Modules:
  0.0 717.8 jit_solution(7056581813542173455)
XLA Ops:
  7.2 5.3 all-to-all-start.1
  14.6 57.9 %all-to-all-done.1 = bf16[4,256,2560]{2,1,0:T(8,128)(2,1)} async-done(((bf16[4,256,2560]{2,1,0:T(8,128)(2,1)}), bf16[4,256,2560]{2,1,0:T(8,128)(2,1)}, u32[]{:S(2)}, u32[]{:S(2)}) %all-to-all-start.1) | async-done | bytes 5242912 | tf_op jit(solution)/shard_map/all_to_all | solution.py:101
  72.5 3.3 all-to-all-start
  75.8 8.0 %copy.52 = bf16[256,4,2560]{0,2,1:T(8,128)(2,1)} copy(bf16[256,4,2560]{2,0,1:T(8,128)(2,1)} %bitcast.6) | data formatting | bytes 10485760 | tf_op jit(solution)/shard_map/all_to_all | solution.py:101
  83.8 121.6 %all_to_all.136 = bf16[256,8,1280]{0,2,1:T(8,128)(2,1)} all-to-all(bf16[256,8,1280]{0,2,1:T(8,128)(2,1)} %bitcast.137), channel_id=1, replica_groups=mesh['dp'=4,'fsdp'=8] {'fsdp'}, dimensions={1} | all-to-all | bytes 10485760 | tf_op jit(solution)/shard_map/all_to_all | solution.py:100
  205.4 4.8 all-to-all-start.5
  210.4 14.0 %all_gather.9 = bf16[8,4,1,2048]{3,1,2,0:T(4,128)(2,1)S(1)} all-gather(bf16[1,4,1,2048]{3,1,2,0:T(4,128)(2,1)S(1)} %broadcast_in_dim_reshape.6), channel_id=1, replica_groups=mesh['dp'=4,'fsdp'=8] {'fsdp'}, dimensions={0}, use_global_device_ids=true | all-gather | bytes 147456 | tf_op jit(solution)/shard_map/all_gather | solution.py:113
  224.3 7.8 %copy.53 = bf16[8,256,1280]{2,1,0:T(8,128)(2,1)} copy(bf16[8,256,1280]{1,2,0:T(8,128)(2,1)} %bitcast.136) | data formatting | bytes 10485760 | tf_op jit(solution)/shard_map/all_to_all | solution.py:100
  232.2 4.1 convolution_bitcast_fusion
  236.3 32.0 %reduce-scatter.9.cloned.1.call-done = f32[8,1,1,1280]{3,0,1,2:T(8,128)} async-done(((f32[8,4,1,1280]{3,0,1,2:T(8,128)}), f32[8,1,1,1280]{3,0,1,2:T(8,128)}) %reduce-scatter.9.cloned.1.call-update) | async-done | bytes 40976
  269.7 4.6 all-to-all-start.3
  274.3 6.2 copy.59
  280.5 5.2 all-to-all-start.6
  289.8 90.0 %all-to-all-done.6 = bf16[256,8,1024]{0,2,1:T(8,128)(2,1)} async-done(((bf16[256,8,1024]{0,2,1:T(8,128)(2,1)}), bf16[256,8,1024]{0,2,1:T(8,128)(2,1)}, u32[]{:S(2)}, u32[]{:S(2)}) %all-to-all-start.6) | async-done | bytes 4194336 | tf_op jit(solution)/shard_map/all_to_all | solution.py:134
  383.1 6.5 copy.60
  389.6 14.0 %all_gather.10 = bf16[8,4,1,2048]{3,1,2,0:T(4,128)(2,1)S(1)} all-gather(bf16[1,4,1,2048]{3,1,2,0:T(4,128)(2,1)S(1)} %broadcast_in_dim_reshape.7), channel_id=1, replica_groups=mesh['dp'=4,'fsdp'=8] {'fsdp'}, dimensions={0}, use_global_device_ids=true | all-gather | bytes 147456 | tf_op jit(solution)/shard_map/all_gather | solution.py:147
  403.6 3.6 convolution_bitcast_fusion.1
  407.2 23.6 %reduce-scatter.11.cloned.1.call-done = f32[8,1,1,1024]{3,0,1,2:T(8,128)} async-done(((f32[8,4,1,1024]{3,0,1,2:T(8,128)}), f32[8,1,1,1024]{3,0,1,2:T(8,128)}) %reduce-scatter.11.cloned.1.call-update) | async-done | bytes 32784
  432.2 4.6 all-to-all-start.7
  437.1 5.5 all-to-all-done.7
  444.0 6.8 copy.62
  451.3 62.6 %reduce.10 = bf16[8192]{0:T(1024)(128)(2,1)S(1)} reduce(bf16[8192,1,1]{2,1,0:T(2,128)(2,1)} %bitcast.139, bf16[]{:T(256)} %broadcast.87), dimensions={1,2}, to_apply=%bitcast.123.reduce_sub_computation | reduce | bytes 32770
  513.9 7.3 %all_to_all.137 = bf16[4,2,1024]{2,1,0:T(2,128)(2,1)S(1)} all-to-all(bf16[4,2,1024]{2,1,0:T(2,128)(2,1)S(1)} %reshape.331), channel_id=1, replica_groups=mesh['dp'=4,'fsdp'=8] {'dp'}, dimensions={0} | all-to-all | bytes 32768 | tf_op jit(solution)/shard_map/all_to_all | solution.py:155
  521.2 5.6 reshape.332
  526.8 62.0 %bitcast_reduce_fusion = bf16[8192]{0:T(1024)(128)(2,1)S(1)} fusion(bf16[8192,1,1]{2,1,0:T(2,128)(2,1)} %reshape.332), kind=kLoop, calls=%fused_computation.73 | loop fusion | bytes 32768 | tf_op jit(solution)/shard_map/all_to_all | solution.py:155
  588.8 14.2 %all_gather.11 = bf16[8,4,1,2048]{3,1,2,0:T(4,128)(2,1)S(1)} all-gather(bf16[1,4,1,2048]{3,1,2,0:T(4,128)(2,1)S(1)} %broadcast_in_dim.53), channel_id=1, replica_groups=mesh['dp'=4,'fsdp'=8] {'fsdp'}, dimensions={0}, use_global_device_ids=true | all-gather | bytes 147456 | tf_op jit(solution)/shard_map/all_gather | solution.py:156
  603.0 7.6 %fusion.12 = bf16[8,4,1,1,3584]{4,0,1,3,2:T(8,128)(2,1)S(1)} fusion(bf16[2048,3584]{1,0:T(8,128)(2,1)} %param.20, bf16[8,4,1,2048]{3,1,2,0:T(4,128)(2,1)S(1)} %all_gather.11), kind=kOutput, calls=%fused_computation.8 | convolution fusion | flops 469876736 | bytes 15040512 | tf_op jit(solution)/shard_map/fask,kn->fasn/dot_general | solution.py:158
  610.6 7.7 %fusion.15 = bf16[8,4,1,1,3584]{4,0,1,3,2:T(8,128)(2,1)S(1)} fusion(bf16[2048,3584]{1,0:T(8,128)(2,1)} %param.19, bf16[8,4,1,2048]{3,1,2,0:T(4,128)(2,1)S(1)} %all_gather.11), kind=kOutput, calls=%fused_computation.9 | convolution fusion | flops 469876736 | bytes 15040512 | tf_op jit(solution)/shard_map/fask,kn->fasn/dot_general | solution.py:157
  619.8 40.7 %all-reduce.6.cloned.1.call-done = bf16[8,4,1,2,3584]{4,0,1,3,2:T(8,128)(2,1)} async-done(((bf16[8,4,1,2,3584]{4,0,1,3,2:T(8,128)(2,1)}), bf16[8,4,1,2,3584]{4,0,1,3,2:T(8,128)(2,1)}) %all-reduce.6.cloned.1.call-update) | async-done | bytes 458768 | tf_op jit(solution)/shard_map/psum | solution.py:160
  661.6 7.7 %fusion.18 = f32[8,4,1,2048]{3,0,1,2:T(8,128)S(1)} fusion(bf16[3584,2048]{1,0:T(8,128)(2,1)} %param.21, f32[8,4,1,2,3584]{4,0,1,3,2:T(8,128)S(1)} %convert_element_type.113), kind=kOutput, calls=%fused_computation.10 | convolution fusion | flops 470450176 | bytes 15859712 | tf_op jit(solution)/shard_map/fask,kn->fasn/dot_general | solution.py:163
  669.5 31.1 %all-reduce.7 = bf16[8,4,1,2048]{3,1,2,0:T(4,128)(2,1)S(1)} all-reduce(f32[8,4,1,2048]{3,1,2,0:T(4,128)S(1)} %copy.64), channel_id=4, replica_groups=mesh['dp'=4,'fsdp'=8] {'fsdp'}, use_global_device_ids=true, to_apply=%region_7.8.clone | all-reduce | flops 65536 | bytes 393216
  706.6 4.0 all-to-all-done.9
  (69 shorter events, 21.8 us)
Async XLA Ops:
  7.2 5.4 copy-start.3
  7.2 5.4 copy-start.2
  7.2 65.4 %all-to-all-start.1 = ((bf16[4,256,2560]{2,1,0:T(8,128)(2,1)}), bf16[4,256,2560]{2,1,0:T(8,128)(2,1)}, u32[]{:S(2)}, u32[]{:S(2)}) async-start(bf16[4,256,2560]{2,1,0:T(8,128)(2,1)} %bitcast.140), calls=%async_computation.1 | async-start | bytes 10485760 | tf_op jit(solution)/shard_map/all_to_all | solution.py:101
  72.5 11.2 %all-to-all-start = ((bf16[1,8,4,256]{3,1,0,2:T(8,128)(2,1)}), bf16[1,8,4,256]{3,1,0,2:T(8,128)(2,1)S(1)}, u32[]{:S(2)}, u32[]{:S(2)}) async-start(bf16[1,8,4,256]{3,1,0,2:T(8,128)(2,1)} %copy.50), calls=%async_computation | async-start | bytes 32768 | tf_op jit(solution)/shard_map/all_to_all | solution.py:107
  205.4 64.3 %all-to-all-start.5 = ((bf16[4,256,2048]{2,1,0:T(8,128)(2,1)}), bf16[4,256,2048]{2,1,0:T(8,128)(2,1)}, u32[]{:S(2)}, u32[]{:S(2)}) async-start(bf16[4,256,2048]{2,1,0:T(8,128)(2,1)} %bitcast.141), calls=%async_computation.5 | async-start | bytes 8388608 | tf_op jit(solution)/shard_map/all_to_all | solution.py:135
  210.3 58.0 %reduce-scatter.9.cloned.1.call-start = ((), (), s32[]{:S(2)}) async-start(), calls=%async_computation.13 | async-start | bytes 204800
  269.7 10.8 %all-to-all-start.3 = ((f32[8,1,1,1280]{3,1,2,0:T(1,128)}), f32[8,1,1,1280]{3,1,2,0:T(1,128)S(1)}, u32[]{:S(2)}, u32[]{:S(2)}) async-start(f32[8,1,1,1280]{3,1,2,0:T(1,128)} %copy.54), calls=%async_computation.3 | async-start | bytes 81920 | tf_op jit(solution)/shard_map/all_to_all | solution.py:118
  280.5 5.9 copy-start
  280.5 6.2 copy-start.1
  280.5 99.3 %all-to-all-start.6 = ((bf16[256,8,1024]{0,2,1:T(8,128)(2,1)}), bf16[256,8,1024]{0,2,1:T(8,128)(2,1)}, u32[]{:S(2)}, u32[]{:S(2)}) async-start(bf16[256,8,1024]{0,2,1:T(8,128)(2,1)} %bitcast.138), calls=%async_computation.6 | async-start | bytes 8388608 | tf_op jit(solution)/shard_map/all_to_all | solution.py:134
  379.8 9.8 %all-to-all-start.4 = ((bf16[1,8,4,256]{3,1,0,2:T(8,128)(2,1)}), bf16[1,8,4,256]{3,1,0,2:T(8,128)(2,1)S(1)}, u32[]{:S(2)}, u32[]{:S(2)}) async-start(bf16[1,8,4,256]{3,1,0,2:T(8,128)(2,1)} %copy.57), calls=%async_computation.4 | async-start | bytes 32768 | tf_op jit(solution)/shard_map/all_to_all | solution.py:141
  383.1 47.8 %reduce-scatter.11.cloned.1.call-start = ((), (), s32[]{:S(2)}) async-start(), calls=%async_computation.14 | async-start | bytes 163840
  389.6 47.5 %copy-start.4 = (bf16[8192]{0:T(1024)(128)(2,1)S(1)}, bf16[8192]{0:T(1024)(128)(2,1)}, u32[]{:S(2)}) copy-start(bf16[8192]{0:T(1024)(128)(2,1)} %param.18) | copy-start | bytes 49156
  432.2 10.3 %all-to-all-start.7 = ((f32[8,1,1,1024]{3,1,2,0:T(1,128)}), f32[8,1,1,1024]{3,1,2,0:T(1,128)S(1)}, u32[]{:S(2)}, u32[]{:S(2)}) async-start(f32[8,1,1,1024]{3,1,2,0:T(1,128)} %copy.61), calls=%async_computation.7 | async-start | bytes 65536 | tf_op jit(solution)/shard_map/all_to_all | solution.py:152
  436.8 223.7 %all-reduce.6.cloned.1.call-start = ((), (), s32[]{:S(2)}) async-start(), calls=%async_computation.12 | async-start | bytes 917504 | tf_op jit(solution)/shard_map/psum | solution.py:160
  610.6 8.5 %copy-start.5 = (u32[32]{0:T(128)S(1)}, u32[32]{0:T(128)}, u32[]{:S(2)}) copy-start(u32[32]{0:T(128)} %constant.44) | copy-start | bytes 388
  702.6 7.9 %all-to-all-start.9 = ((bf16[4,2,1024]{2,1,0:T(2,128)(2,1)}), bf16[4,2,1024]{2,1,0:T(2,128)(2,1)S(1)}, u32[]{:S(2)}, u32[]{:S(2)}) async-start(bf16[4,2,1024]{2,1,0:T(2,128)(2,1)} %reshape.333), calls=%async_computation.9 | async-start | bytes 32768 | tf_op jit(solution)/shard_map/all_to_all | solution.py:168
Sparse Core Ops, SparseCore 0:
  236.4 31.7 reduce-scatter.8
  407.3 23.4 reduce-scatter.10
  619.3 41.1 all-reduce.5
where the time goes:
time: 720 us; the launch traced here: 718 us
  waiting for transfers between devices  254 us (35%)
  blocking collectives  202 us (28%)
  local copies, waits for them, and re-layouts  111 us (15%)
  other arithmetic  68.6 us (10%)
  starting transfers between devices  34.7 us (5%)
  matrix products  31.7 us (4%)
  between operations  16 us (2%)
    all_to_all x1, blocking collectives, on_device(): lax.all_to_all(lax.all_to_all(w_qkv, 'dp', split_axis=0, concat_axis=1, t...  122 us
    all_to_all x1, waiting for transfers between devices, on_device(): lax.all_to_all(lax.all_to_all(w_out, 'dp', split_axis=0, concat_axis=1, t...  90 us
    unnamed x3, other arithmetic  63.4 us
    all_to_all x1, local copies, waits for them, and re-layouts, on_device(): lax.all_to_all(normed_mid[None], 'dp', split_axis=2, concat_axis=0, tiled...  62 us
    all_to_all x1, waiting for transfers between devices, on_device(): lax.all_to_all(w_qkv, 'dp', split_axis=0, concat_axis=1, tiled=True)  57.9 us
    unnamed x5, waiting for transfers between devices  55.7 us
    psum x1, waiting for transfers between devices, on_device(): summed = lax.psum(partials.astype(jnp.bfloat16), 'dp').astype(jnp.float32)  40.7 us
    unnamed x1, blocking collectives  31.1 us
  transfers between devices with their start and end apart: 11, of which 7 were waited for; matrix products, arithmetic and copies ran while one was open for 6% of the time, Pallas kernels for 0%

commit v1 on v0

--- a/solution.py
+++ b/solution.py
@@ -131,12 +131,20 @@
         value_cache,
         lengths,
     )
-    out_tile = lax.all_to_all(
-        lax.all_to_all(w_out, "dp", split_axis=0, concat_axis=1, tiled=True),
-        "fsdp",
-        split_axis=1,
-        concat_axis=0,
-        tiled=True,
+    out_tile = jnp.concatenate(
+        lax.all_to_all(
+            jnp.stack(
+                jnp.split(
+                    lax.all_to_all(w_out, "dp", split_axis=0, concat_axis=1, tiled=True),
+                    lax.axis_size("fsdp"),
+                    axis=1,
+                )
+            ),
+            "fsdp",
+            0,
+            0,
+        ),
+        axis=0,
     )
     out_moved = lax.all_to_all(
         quarter_split(mixed, dp_size, fsdp_size), "dp", split_axis=2, concat_axis=0, tiled=True

time: 720 us -> 747 us (1.038)
  blocking collectives: 202 us -> 348 us
  waiting for transfers between devices: 254 us -> 136 us
    all_to_all x3 -> x2, waiting for transfers between devices: 148 us -> 0.01 us  [the longest x1 0.01 us: on_device(): lax.all_to_all(lax.all_to_all(w_qkv, 'dp', split_axis=0, concat_axis=1, t...]
    all_gather x1, blocking collectives: 14 us -> 121 us  [on_device(): lax.all_gather(qkv_in, 'fsdp', axis=0, tiled=True)]
    all_gather x1, blocking collectives: 14 us -> 100 us  [on_device(): lax.all_gather(out_in, 'fsdp', axis=0, tiled=True)]
    all_to_all x1 -> x2, blocking collectives: 122 us -> 73.7 us  [the longest x1 64 us: on_device(): lax.all_to_all(w_qkv, 'dp', split_axis=0, concat_axis=1, tiled=True)]
    all_to_all x1, waiting for transfers between devices: 0.01 us -> 36.9 us  [on_device(): lax.all_to_all(w_out, 'dp', split_axis=0, concat_axis=1, tiled=True)]
    unnamed x5, waiting for transfers between devices: 55.7 us -> 42.6 us
    unnamed x21 -> x28, local copies, waits for them, and re-layouts: 8.48 us -> 18.1 us
  transfers between devices with their start and end apart: 11 -> 10, of which waited for: 7 -> 8; matrix products, arithmetic and copies ran while one was open for 6% -> 3% of each run, Pallas kernels for 0% -> 0%
where the time goes in v1:
time: 747 us; the launch traced here: 745 us
  blocking collectives  348 us (47%)
  waiting for transfers between devices  136 us (18%)
  local copies, waits for them, and re-layouts  111 us (15%)
  other arithmetic  70.9 us (9%)
  matrix products  31.7 us (4%)
  starting transfers between devices  30.4 us (4%)
  between operations  16 us (2%)
    all_gather x1, blocking collectives, on_device(): lax.all_gather(qkv_in, 'fsdp', axis=0, tiled=True)  121 us
    all_gather x1, blocking collectives, on_device(): lax.all_gather(out_in, 'fsdp', axis=0, tiled=True)  100 us
    all_to_all x1, blocking collectives, on_device(): lax.all_to_all(w_qkv, 'dp', split_axis=0, concat_axis=1, tiled=True)  64 us
    unnamed x3, other arithmetic  63.4 us
    all_to_all x1, local copies, waits for them, and re-layouts, on_device(): lax.all_to_all(normed_mid[None], 'dp', split_axis=2, concat_axis=0, tiled...  62 us
    unnamed x5, waiting for transfers between devices  42.6 us
    psum x1, waiting for transfers between devices, on_device(): summed = lax.psum(partials.astype(jnp.bfloat16), 'dp').astype(jnp.float32)  40.7 us
    all_to_all x1, waiting for transfers between devices, on_device(): lax.all_to_all(w_out, 'dp', split_axis=0, concat_axis=1, tiled=True)  36.9 us
  transfers between devices with their start and end apart: 10, of which 8 were waited for; matrix products, arithmetic and copies ran while one was open for 3% of the time, Pallas kernels for 0%

profile of v1, /device:TPU:0, one launch (start us, length us, event | category | flops | bytes accessed | tf_op | source)
XLA Modules:
  0.0 744.8 jit_solution(15578926886328867678)
XLA Ops:
  10.9 9.7 %all_to_all.125 = bf16[1,8,4,256]{3,1,0,2:T(8,128)(2,1)S(1)} all-to-all(bf16[1,8,4,256]{3,1,0,2:T(8,128)(2,1)S(1)} %copy.49), channel_id=1, replica_groups=mesh['dp'=4,'fsdp'=8] {'dp'}, dimensions={2} | all-to-all | bytes 32768 | tf_op jit(solution)/shard_map/all_to_all | solution.py:107
  20.6 64.0 %all_to_all.126 = bf16[4,256,2560]{2,1,0:T(8,128)(2,1)} all-to-all(bf16[4,256,2560]{2,1,0:T(8,128)(2,1)} %bitcast.178), channel_id=1, replica_groups=mesh['dp'=4,'fsdp'=8] {'dp'}, dimensions={0} | all-to-all | bytes 10485760 | tf_op jit(solution)/shard_map/all_to_all | solution.py:101
  84.6 4.8 all-to-all-start.5
  89.5 7.9 %copy.51 = bf16[256,4,2560]{0,2,1:T(8,128)(2,1)} copy(bf16[256,4,2560]{2,0,1:T(8,128)(2,1)} %bitcast.168) | data formatting | bytes 10485760 | tf_op jit(solution)/shard_map/all_to_all | solution.py:101
  97.4 36.9 %all-to-all-done.5 = bf16[4,256,2048]{2,1,0:T(8,128)(2,1)} async-done(((bf16[4,256,2048]{2,1,0:T(8,128)(2,1)}), bf16[4,256,2048]{2,1,0:T(8,128)(2,1)}, u32[]{:S(2)}, u32[]{:S(2)}) %all-to-all-start.5) | async-done | bytes 4194336 | tf_op jit(solution)/shard_map/all_to_all | solution.py:138
  134.3 5.0 all-to-all-start.2
  140.7 121.5 %all_gather.9 = bf16[8,4,1,2048]{3,1,2,0:T(4,128)(2,1)S(1)} all-gather(bf16[1,4,1,2048]{3,1,2,0:T(4,128)(2,1)S(1)} %broadcast_in_dim_reshape.6), channel_id=1, replica_groups=mesh['dp'=4,'fsdp'=8] {'fsdp'}, dimensions={0}, use_global_device_ids=true | all-gather | bytes 147456 | tf_op jit(solution)/shard_map/all_gather | solution.py:113
  268.7 7.8 %copy.52 = bf16[8,256,1280]{2,1,0:T(8,128)(2,1)} copy(bf16[8,256,1280]{1,2,0:T(8,128)(2,1)} %bitcast.8) | data formatting | bytes 10485760 | tf_op jit(solution)/shard_map/all_to_all | solution.py:100
  276.5 4.1 convolution_bitcast_fusion
  284.4 19.9 %reduce-scatter.9.cloned.1.call-done = f32[8,1,1,1280]{3,0,1,2:T(8,128)} async-done(((f32[8,4,1,1280]{3,0,1,2:T(8,128)}), f32[8,1,1,1280]{3,0,1,2:T(8,128)}) %reduce-scatter.9.cloned.1.call-update) | async-done | bytes 40976
  305.7 4.6 all-to-all-start.3
  312.2 3.9 all-to-all-done.3
  318.8 3.3 all-to-all-start.4
  326.7 4.5 all-to-all-start.6
  331.4 100.1 %all_gather.10 = bf16[8,4,1,2048]{3,1,2,0:T(4,128)(2,1)S(1)} all-gather(bf16[1,4,1,2048]{3,1,2,0:T(4,128)(2,1)S(1)} %broadcast_in_dim_reshape.7), channel_id=1, replica_groups=mesh['dp'=4,'fsdp'=8] {'fsdp'}, dimensions={0}, use_global_device_ids=true | all-gather | bytes 147456 | tf_op jit(solution)/shard_map/all_gather | solution.py:155
  431.5 3.6 convolution_bitcast_fusion.1
  435.1 22.7 %reduce-scatter.11.cloned.1.call-done = f32[8,1,1,1024]{3,0,1,2:T(8,128)} async-done(((f32[8,4,1,1024]{3,0,1,2:T(8,128)}), f32[8,1,1,1024]{3,0,1,2:T(8,128)}) %reduce-scatter.11.cloned.1.call-update) | async-done | bytes 32784
  459.3 4.6 all-to-all-start.7
  464.1 5.5 all-to-all-done.7
  471.0 6.8 copy.60
  478.3 62.6 %reduce.10 = bf16[8192]{0:T(1024)(128)(2,1)S(1)} reduce(bf16[8192,1,1]{2,1,0:T(2,128)(2,1)} %bitcast.177, bf16[]{:T(256)} %broadcast.87), dimensions={1,2}, to_apply=%bitcast.155.reduce_sub_computation | reduce | bytes 32770
  541.0 7.3 all_to_all.127
  548.2 5.6 reshape.332
  553.8 62.0 %bitcast_reduce_fusion = bf16[8192]{0:T(1024)(128)(2,1)S(1)} fusion(bf16[8192,1,1]{2,1,0:T(2,128)(2,1)} %reshape.332), kind=kLoop, calls=%fused_computation.89 | loop fusion | bytes 32768 | tf_op jit(solution)/shard_map/all_to_all | solution.py:163
  615.8 14.2 %all_gather.11 = bf16[8,4,1,2048]{3,1,2,0:T(4,128)(2,1)S(1)} all-gather(bf16[1,4,1,2048]{3,1,2,0:T(4,128)(2,1)S(1)} %broadcast_in_dim.53), channel_id=1, replica_groups=mesh['dp'=4,'fsdp'=8] {'fsdp'}, dimensions={0}, use_global_device_ids=true | all-gather | bytes 147456 | tf_op jit(solution)/shard_map/all_gather | solution.py:164
  630.0 7.6 %fusion.12 = bf16[8,4,1,1,3584]{4,0,1,3,2:T(8,128)(2,1)S(1)} fusion(bf16[2048,3584]{1,0:T(8,128)(2,1)} %param.20, bf16[8,4,1,2048]{3,1,2,0:T(4,128)(2,1)S(1)} %all_gather.11), kind=kOutput, calls=%fused_computation.8 | convolution fusion | flops 469876736 | bytes 15040512 | tf_op jit(solution)/shard_map/fask,kn->fasn/dot_general | solution.py:166
  637.7 7.7 %fusion.15 = bf16[8,4,1,1,3584]{4,0,1,3,2:T(8,128)(2,1)S(1)} fusion(bf16[2048,3584]{1,0:T(8,128)(2,1)} %param.19, bf16[8,4,1,2048]{3,1,2,0:T(4,128)(2,1)S(1)} %all_gather.11), kind=kOutput, calls=%fused_computation.9 | convolution fusion | flops 469876736 | bytes 15040512 | tf_op jit(solution)/shard_map/fask,kn->fasn/dot_general | solution.py:165
  646.8 40.7 %all-reduce.6.cloned.1.call-done = bf16[8,4,1,2,3584]{4,0,1,3,2:T(8,128)(2,1)} async-done(((bf16[8,4,1,2,3584]{4,0,1,3,2:T(8,128)(2,1)}), bf16[8,4,1,2,3584]{4,0,1,3,2:T(8,128)(2,1)}) %all-reduce.6.cloned.1.call-update) | async-done | bytes 458768 | tf_op jit(solution)/shard_map/psum | solution.py:168
  688.6 7.7 %fusion.18 = f32[8,4,1,2048]{3,0,1,2:T(8,128)S(1)} fusion(bf16[3584,2048]{1,0:T(8,128)(2,1)} %param.21, f32[8,4,1,2,3584]{4,0,1,3,2:T(8,128)S(1)} %convert_element_type.113), kind=kOutput, calls=%fused_computation.10 | convolution fusion | flops 470450176 | bytes 15859712 | tf_op jit(solution)/shard_map/fask,kn->fasn/dot_general | solution.py:171
  696.5 31.1 %all-reduce.7 = bf16[8,4,1,2048]{3,1,2,0:T(4,128)(2,1)S(1)} all-reduce(f32[8,4,1,2048]{3,1,2,0:T(4,128)S(1)} %copy.62), channel_id=4, replica_groups=mesh['dp'=4,'fsdp'=8] {'fsdp'}, use_global_device_ids=true, to_apply=%region_7.8.clone | all-reduce | flops 65536 | bytes 393216
  729.6 3.3 all-to-all-start.9
  733.6 4.0 all-to-all-done.9
  (75 shorter events, 33.7 us)
Async XLA Ops:
  84.6 49.7 %all-to-all-start.5 = ((bf16[4,256,2048]{2,1,0:T(8,128)(2,1)}), bf16[4,256,2048]{2,1,0:T(8,128)(2,1)}, u32[]{:S(2)}, u32[]{:S(2)}) async-start(bf16[4,256,2048]{2,1,0:T(8,128)(2,1)} %bitcast.179), calls=%async_computation.5 | async-start | bytes 8388608 | tf_op jit(solution)/shard_map/all_to_all | solution.py:138
  134.3 5.7 copy-start.1
  134.3 6.0 copy-start.2
  134.3 134.3 %all-to-all-start.2 = ((bf16[256,8,1280]{0,2,1:T(8,128)(2,1)}), bf16[256,8,1280]{0,2,1:T(8,128)(2,1)}, u32[]{:S(2)}, u32[]{:S(2)}) async-start(bf16[256,8,1280]{0,2,1:T(8,128)(2,1)} %bitcast.167), calls=%async_computation.2 | async-start | bytes 10485760 | tf_op jit(solution)/shard_map/all_to_all | solution.py:100
  139.3 164.9 %reduce-scatter.9.cloned.1.call-start = ((), (), s32[]{:S(2)}) async-start(), calls=%async_computation.13 | async-start | bytes 204800
  264.7 3.1 copy-start
  305.7 10.4 %all-to-all-start.3 = ((f32[8,1,1,1280]{3,1,2,0:T(1,128)}), f32[8,1,1,1280]{3,1,2,0:T(1,128)S(1)}, u32[]{:S(2)}, u32[]{:S(2)}) async-start(f32[8,1,1,1280]{3,1,2,0:T(1,128)} %copy.53), calls=%async_computation.3 | async-start | bytes 81920 | tf_op jit(solution)/shard_map/all_to_all | solution.py:118
  318.8 7.9 %all-to-all-start.4 = ((bf16[1,8,4,256]{3,1,0,2:T(8,128)(2,1)}), bf16[1,8,4,256]{3,1,0,2:T(8,128)(2,1)S(1)}, u32[]{:S(2)}, u32[]{:S(2)}) async-start(bf16[1,8,4,256]{3,1,0,2:T(8,128)(2,1)} %copy.56), calls=%async_computation.4 | async-start | bytes 32768 | tf_op jit(solution)/shard_map/all_to_all | solution.py:149
  326.7 104.8 %all-to-all-start.6 = ((bf16[8,256,1024]{2,1,0:T(8,128)(2,1)}), bf16[8,256,1024]{2,1,0:T(8,128)(2,1)}, u32[]{:S(2)}, u32[]{:S(2)}) async-start(bf16[8,256,1024]{2,1,0:T(8,128)(2,1)} %fusion.25), calls=%async_computation.6 | async-start | bytes 8388608 | tf_op jit(solution)/shard_map/all_to_all | solution.py:135
  331.3 132.8 %copy-start.4 = (bf16[8192]{0:T(1024)(128)(2,1)S(1)}, bf16[8192]{0:T(1024)(128)(2,1)}, u32[]{:S(2)}) copy-start(bf16[8192]{0:T(1024)(128)(2,1)} %param.18) | copy-start | bytes 49156
  331.3 138.3 %copy-start.3 = (bf16[1,8192]{1,0:T(2,128)(2,1)S(1)}, bf16[1,8192]{1,0:T(2,128)(2,1)}, u32[]{:S(2)}) copy-start(bf16[1,8192]{1,0:T(2,128)(2,1)} %param.11) | copy-start | bytes 49156
  331.3 126.5 %reduce-scatter.11.cloned.1.call-start = ((), (), s32[]{:S(2)}) async-start(), calls=%async_computation.14 | async-start | bytes 163840
  459.3 10.3 %all-to-all-start.7 = ((f32[8,1,1,1024]{3,1,2,0:T(1,128)}), f32[8,1,1,1024]{3,1,2,0:T(1,128)S(1)}, u32[]{:S(2)}, u32[]{:S(2)}) async-start(f32[8,1,1,1024]{3,1,2,0:T(1,128)} %copy.59), calls=%async_computation.7 | async-start | bytes 65536 | tf_op jit(solution)/shard_map/all_to_all | solution.py:160
  463.8 223.7 %all-reduce.6.cloned.1.call-start = ((), (), s32[]{:S(2)}) async-start(), calls=%async_computation.12 | async-start | bytes 917504 | tf_op jit(solution)/shard_map/psum | solution.py:168
  637.6 8.5 %copy-start.5 = (u32[32]{0:T(128)S(1)}, u32[32]{0:T(128)}, u32[]{:S(2)}) copy-start(u32[32]{0:T(128)} %constant.44) | copy-start | bytes 388
  729.6 7.9 %all-to-all-start.9 = ((bf16[4,2,1024]{2,1,0:T(2,128)(2,1)}), bf16[4,2,1024]{2,1,0:T(2,128)(2,1)S(1)}, u32[]{:S(2)}, u32[]{:S(2)}) async-start(bf16[4,2,1024]{2,1,0:T(2,128)(2,1)} %reshape.333), calls=%async_computation.9 | async-start | bytes 32768 | tf_op jit(solution)/shard_map/all_to_all | solution.py:176
Sparse Core Ops, SparseCore 0:
  280.7 23.4 reduce-scatter.8
  435.2 22.5 reduce-scatter.10
  646.3 41.1 all-reduce.5
